TPU v7x, 32 devices: a whole 2x2x4 slice. The times are simulated.
32 devices in a mesh: vocab: 8 (over y, x, core), dp: 4 (over z).
Axes of the slice: x: 2, y: 2, z: 4, core: 2. Of those that a mesh axis runs over, the one named last changes fastest.
Arguments:
- token_ids: int32 [8192], P(('vocab', 'dp')), may hold values from 0 to 50256
- target_ids: int32 [8192], P(('vocab', 'dp')), may hold values from 0 to 50256
- loss_mask: int32 [8192], P(('vocab', 'dp')), may hold values from 0 to 1, as said below
- seq_ids: int32 [8192], P(('vocab', 'dp')), may hold values from 0 to 255, as said below
- embed_table: bfloat16 [50304, 1024], P('vocab'), may hold values from -0.359375 to 0.359375
- pos_table: bfloat16 [1024, 1024], replicated, may hold values from -0.359375 to 0.359375
- gains: float32 [3, 1024], replicated, may hold values from 0.5 to 1.5
- shifts: float32 [3, 1024], replicated, may hold values from -1.8 to 1.8
- linear_bias: float32 [1, 9216], replicated, may hold values from -1.8 to 1.8
- query_key_value_weight: bfloat16 [1, 1024, 3072], replicated, may hold values from -0.1875 to 0.1875
- w_out: bfloat16 [1, 1024, 1024], replicated, may hold values from -0.5 to 0.5
- w_fc: bfloat16 [1, 1024, 4096], replicated, may hold values from -0.1875 to 0.1875
- w_proj: bfloat16 [1, 4096, 1024], replicated, may hold values from -0.09375 to 0.09375
- adapters: float32 [1, 24576], P(None, 'vocab'), may hold values from -0.18 to 0.18
- first_moment: float32 [1, 24576], P(None, 'vocab'), may hold values from -4.2483338e-05 to 4.2483338e-05
- second_moment: float32 [1, 24576], P(None, 'vocab'), may hold values from 2.0345052e-12 to 3.2552083e-11
- step_count: int32 [1], replicated, may hold values from 2 to 20
Outputs:
- loss: float32 [], replicated
- grad_norm: float32 [], replicated
- new_adapters: float32 [1, 24576], P(None, 'vocab')
- new_first: float32 [1, 24576], P(None, 'vocab')
- new_second: float32 [1, 24576], P(None, 'vocab')
- adapter_copy: bfloat16 [1, 24576], P(None, 'vocab')
Inputs may be any that keep to these rules, and one draw needn't show every extreme that they name: seq_ids never falls; the tokens of each device form whole sequences of 256 // 8 times 1, 2, 4 or 8 tokens, each starting at a multiple of its length within the device; some device holds one sequence of 256 tokens and some device eight of 32. `token_ids`: every id is a real row, below 50257. `target_ids`: every target is a real row, below 50257. `loss_mask`: the share of ones differs from device to device; some devices have all ones.
All inputs are finite; a program needn't handle non-finite values.
Results may differ from a plain program's by a relative error of at most 0.0051.
Values may be sent and summed in bfloat16 or wider, within the bound.
A program may use at most 256 MiB of HBM per device.

v0:
```python
import jax
import jax.numpy as jnp
from jax import lax
from jax.sharding import PartitionSpec as P

MODEL_WIDTH = 1024
HEADS = 16
HEAD_DIM = 64
FF = 4096
VOCAB_REAL = 50257
RANK = 4
LAYERS = 1
TOK_DEV = 256
PRECISE = lax.Precision.HIGHEST
ADAPTER_SCALE = 8.0
CLIP_NORM = 0.01
BETA_ONE = 0.9
BETA_TWO = 0.999
ADAM_EPS = 1e-08
WEIGHT_DECAY = 0.01
LEARN_RATE = 0.02


def mixed_product(left, right):
    return jnp.dot(left, right, preferred_element_type=jnp.float32)


def exact_product(left, right):
    return jnp.dot(left.astype(jnp.float32), right.astype(jnp.float32), precision=PRECISE)


def layer_norm(values, gain, shift):
    center = values - jnp.mean(values, -1, keepdims=True)
    spread = jnp.mean(center * center, -1, keepdims=True)
    inverse = lax.rsqrt(spread + 1e-05)
    normed = center * inverse
    return (normed * gain + shift, normed, inverse)


def norm_back(grad_in, normed, inverse, gain):
    scaled = grad_in * gain
    return inverse * (
        scaled
        - jnp.mean(scaled, -1, keepdims=True)
        - normed * jnp.mean(scaled * normed, -1, keepdims=True)
    )


def gelu(values):
    return (
        0.5
        * values
        * (1.0 + jnp.tanh(0.7978845608028654 * (values + 0.044715 * values * values * values)))
    )


def positions_of(seq):
    place = jnp.arange(seq.shape[0], dtype=jnp.int32)
    fresh = jnp.concatenate([jnp.ones((1,), bool), seq[1:] != seq[:-1]])
    start = lax.cummax(jnp.where(fresh, place, 0))
    return place - start


def split_adapter(flat):
    width = MODEL_WIDTH * RANK
    qkv_down_matrix = flat[:width].reshape(MODEL_WIDTH, RANK)
    output_down_matrix = flat[width : 2 * width].reshape(MODEL_WIDTH, RANK)
    qkv_up_matrix = flat[2 * width : 5 * width].reshape(RANK, 3 * MODEL_WIDTH)
    output_up_matrix = flat[5 * width :].reshape(RANK, MODEL_WIDTH)
    return (qkv_down_matrix, output_down_matrix, qkv_up_matrix, output_up_matrix)


def split_heads(query_key_value):
    count = query_key_value.shape[0]
    query = query_key_value[:, :MODEL_WIDTH].reshape(count, HEADS, HEAD_DIM)
    keys = query_key_value[:, MODEL_WIDTH : 2 * MODEL_WIDTH].reshape(count, HEADS, HEAD_DIM)
    values = query_key_value[:, 2 * MODEL_WIDTH :].reshape(count, HEADS, HEAD_DIM)
    return (query, keys, values)


def attention_forward(query_key_value, visible):
    query, keys, values = split_heads(query_key_value)
    scores = jnp.einsum("qhd,khd->hqk", query, keys, preferred_element_type=jnp.float32) * 0.125
    scores = jnp.where(visible[None], scores, -1e30)
    row_top = jnp.max(scores, -1, keepdims=True)
    expd = jnp.exp(scores - row_top)
    row_total = jnp.sum(expd, -1, keepdims=True)
    probs = (expd / row_total).astype(jnp.bfloat16)
    attention_output = jnp.einsum("hqk,khd->qhd", probs, values, preferred_element_type=jnp.float32)
    return (
        attention_output.reshape(query_key_value.shape[0], MODEL_WIDTH),
        row_top + jnp.log(row_total),
    )


def attention_back(query_key_value, visible, row_lse, attention_output_gradient):
    query, keys, values = split_heads(query_key_value)
    count = query_key_value.shape[0]
    scores = jnp.einsum("qhd,khd->hqk", query, keys, preferred_element_type=jnp.float32) * 0.125
    probs = jnp.where(visible[None], jnp.exp(scores - row_lse), 0.0)
    grad_heads = attention_output_gradient.reshape(count, HEADS, HEAD_DIM)
    grad_probs = jnp.einsum("qhd,khd->hqk", grad_heads, values, preferred_element_type=jnp.float32)
    grad_values = jnp.einsum(
        "hqk,qhd->khd", probs.astype(jnp.bfloat16), grad_heads, preferred_element_type=jnp.float32
    )
    grad_scores = probs * (grad_probs - jnp.sum(probs * grad_probs, -1, keepdims=True))
    grad_scores = grad_scores.astype(jnp.bfloat16)
    grad_query = (
        jnp.einsum("hqk,khd->qhd", grad_scores, keys, preferred_element_type=jnp.float32) * 0.125
    )
    grad_keys = (
        jnp.einsum("hqk,qhd->khd", grad_scores, query, preferred_element_type=jnp.float32) * 0.125
    )
    joined = jnp.concatenate(
        [
            grad_query.reshape(count, MODEL_WIDTH),
            grad_keys.reshape(count, MODEL_WIDTH),
            grad_values.reshape(count, MODEL_WIDTH),
        ],
        axis=1,
    )
    return joined.astype(jnp.bfloat16)


def local(
    token_ids,
    target_ids,
    loss_mask,
    seq_ids,
    embed_table,
    pos_table,
    gains,
    shifts,
    linear_bias,
    query_key_value_weight,
    w_out,
    w_fc,
    w_proj,
    adapters,
    first_moment,
    second_moment,
    step_count,
):
    vocab_place = lax.axis_index("vocab")
    vocab_count = lax.axis_size("vocab")
    total_tokens = TOK_DEV * vocab_count * lax.axis_size("dp")
    shard_rows = embed_table.shape[0]
    all_tokens, all_targets, all_mask = (
        lax.all_gather(token_ids, "vocab", axis=0, tiled=True),
        lax.all_gather(target_ids, "vocab", axis=0, tiled=True),
        lax.all_gather(loss_mask, "vocab", axis=0, tiled=True),
    )
    mask_weights = all_mask.astype(jnp.float32)
    wanted = all_tokens - vocab_place * shard_rows
    inside = (wanted >= 0) & (wanted < shard_rows)
    picked_rows = jnp.take(embed_table, jnp.clip(wanted, 0, shard_rows - 1), axis=0)
    embedded = lax.psum_scatter(
        jnp.where(inside[:, None], picked_rows.astype(jnp.float32), 0.0).astype(jnp.bfloat16),
        "vocab",
        scatter_dimension=0,
        tiled=True,
    ).astype(jnp.float32)
    copies = lax.all_gather(adapters.astype(jnp.bfloat16), "vocab", axis=1, tiled=True)
    resid = embedded + pos_table[positions_of(seq_ids)].astype(jnp.float32)
    place = jnp.arange(TOK_DEV)
    visible = (seq_ids[:, None] == seq_ids[None, :]) & (place[None, :] <= place[:, None])
    layer_params = 0
    qkv_down_matrix, output_down_matrix, qkv_up_matrix, output_up_matrix = split_adapter(
        copies[layer_params]
    )
    bias_vector = linear_bias[layer_params]
    hidden_first, normed_one, inverse_one = layer_norm(
        resid, gains[2 * layer_params], shifts[2 * layer_params]
    )
    hidden_first = hidden_first.astype(jnp.bfloat16)
    adapter_input = mixed_product(hidden_first, qkv_down_matrix).astype(jnp.bfloat16)
    query_key_value = (
        mixed_product(hidden_first, query_key_value_weight[layer_params])
        + bias_vector[: 3 * MODEL_WIDTH]
        + ADAPTER_SCALE * mixed_product(adapter_input, qkv_up_matrix)
    )
    query_key_value = query_key_value.astype(jnp.bfloat16)
    attention_output, row_lse = attention_forward(query_key_value, visible)
    attention_output = attention_output.astype(jnp.bfloat16)
    adapter_middle = mixed_product(attention_output, output_down_matrix).astype(jnp.bfloat16)
    resid = (
        resid
        + mixed_product(attention_output, w_out[layer_params])
        + bias_vector[3 * MODEL_WIDTH : 4 * MODEL_WIDTH]
        + ADAPTER_SCALE * mixed_product(adapter_middle, output_up_matrix)
    )
    h_two, normed_two, inverse_two = layer_norm(
        resid, gains[2 * layer_params + 1], shifts[2 * layer_params + 1]
    )
    h_two = h_two.astype(jnp.bfloat16)
    pre = (
        mixed_product(h_two, w_fc[layer_params])
        + bias_vector[4 * MODEL_WIDTH : 4 * MODEL_WIDTH + FF]
    )
    act = gelu(pre).astype(jnp.bfloat16)
    resid = resid + mixed_product(act, w_proj[layer_params]) + bias_vector[4 * MODEL_WIDTH + FF :]
    saved = [
        (
            hidden_first,
            normed_one,
            inverse_one,
            adapter_input,
            query_key_value,
            row_lse,
            attention_output,
            adapter_middle,
            normed_two,
            inverse_two,
            pre,
        )
    ]
    hidden, normed_last, inverse_last = layer_norm(resid, gains[2 * LAYERS], shifts[2 * LAYERS])
    hidden = hidden.astype(jnp.bfloat16)
    columns = vocab_place * shard_rows + jnp.arange(shard_rows)
    live = columns < VOCAB_REAL

    def head_logits(row_block):
        logits = jnp.einsum("td,vd->tv", row_block, embed_table, preferred_element_type=jnp.float32)
        return jnp.where(live[None], logits, -1e30)

    piece = lax.all_gather(hidden, "vocab", axis=0, tiled=True)
    logits = head_logits(piece)
    row_top = jnp.max(logits, -1)
    row_total = jnp.sum(jnp.exp(logits - row_top[:, None]), -1)
    wanted = all_targets
    picked = jnp.sum(jnp.where(columns[None, :] == wanted[:, None], logits, 0.0), -1)
    gathered, row_top, row_total, picked = (piece, row_top, row_total, picked)
    joint_top = lax.pmax(row_top, "vocab")
    row_total = row_total * jnp.exp(row_top - joint_top)
    row_total, picked = lax.psum((row_total, picked), "vocab")
    row_lse = joint_top + jnp.log(row_total)
    loss_part = jnp.sum(mask_weights * (row_lse - picked))
    row_block = gathered
    logits = head_logits(row_block)
    wanted = all_targets
    hit = (columns[None, :] == wanted[:, None]).astype(jnp.float32)
    grad_logits = (
        mask_weights[:, None] * (jnp.exp(logits - row_lse[:, None]) - hit) * (1.0 / total_tokens)
    ).astype(jnp.bfloat16)
    grad_hidden = lax.psum_scatter(
        mixed_product(grad_logits, embed_table), "vocab", scatter_dimension=0, tiled=True
    )
    grad_resid = norm_back(grad_hidden, normed_last, inverse_last, gains[2 * LAYERS])
    layer_grads = []
    for layer_params in reversed(range(LAYERS)):
        (
            hidden_first,
            normed_one,
            inverse_one,
            adapter_input,
            query_key_value,
            row_lse_l,
            attention_output,
            adapter_middle,
            normed_two,
            inverse_two,
            pre,
        ) = saved[layer_params]
        qkv_down_matrix, output_down_matrix, qkv_up_matrix, output_up_matrix = split_adapter(
            copies[layer_params]
        )
        grad_top = grad_resid.astype(jnp.bfloat16)
        grad_act = jnp.einsum(
            "te,fe->tf", grad_top, w_proj[layer_params], preferred_element_type=jnp.float32
        )
        grad_pre = jax.vjp(gelu, pre)[1](grad_act)[0].astype(jnp.bfloat16)
        grad_h_two = jnp.einsum(
            "tf,df->td", grad_pre, w_fc[layer_params], preferred_element_type=jnp.float32
        )
        grad_resid = grad_resid + norm_back(
            grad_h_two, normed_two, inverse_two, gains[2 * layer_params + 1]
        )
        middle_gradient = grad_resid.astype(jnp.bfloat16)
        adapter_middle_gradient = ADAPTER_SCALE * jnp.einsum(
            "te,re->tr", middle_gradient, output_up_matrix, preferred_element_type=jnp.float32
        )
        output_up_gradient = ADAPTER_SCALE * jnp.einsum(
            "iz,iq->zq", adapter_middle, middle_gradient, preferred_element_type=jnp.float32
        )
        output_down_gradient = exact_product(attention_output.T, adapter_middle_gradient)
        attention_output_gradient = jnp.einsum(
            "te,de->td", middle_gradient, w_out[layer_params], preferred_element_type=jnp.float32
        )
        attention_output_gradient = (
            attention_output_gradient + exact_product(adapter_middle_gradient, output_down_matrix.T)
        ).astype(jnp.bfloat16)
        query_key_value_gradient = attention_back(
            query_key_value, visible, row_lse_l, attention_output_gradient
        )
        qkv_up_gradient = ADAPTER_SCALE * jnp.einsum(
            "iz,iq->zq", adapter_input, query_key_value_gradient, preferred_element_type=jnp.float32
        )
        adapter_input_gradient = ADAPTER_SCALE * jnp.einsum(
            "te,re->tr", query_key_value_gradient, qkv_up_matrix, preferred_element_type=jnp.float32
        )
        qkv_down_gradient = exact_product(hidden_first.T, adapter_input_gradient)
        layer_grads.insert(
            0,
            jnp.concatenate(
                [
                    qkv_down_gradient.reshape(-1),
                    output_down_gradient.reshape(-1),
                    qkv_up_gradient.reshape(-1),
                    output_up_gradient.reshape(-1),
                ]
            ),
        )
    local_grads = jnp.stack(layer_grads)
    grad_shard = lax.psum_scatter(local_grads, "vocab", scatter_dimension=1, tiled=True)
    grad_shard, loss_sum = lax.psum((grad_shard, loss_part), "dp")
    square_sum = lax.psum(jnp.sum(grad_shard * grad_shard), "vocab")
    loss = loss_sum / total_tokens
    grad_norm = jnp.sqrt(square_sum)
    clipped = grad_shard * jnp.minimum(1.0, CLIP_NORM / (grad_norm + 1e-06))
    step = step_count[0].astype(jnp.float32)
    new_first = BETA_ONE * first_moment + (1.0 - BETA_ONE) * clipped
    new_second = BETA_TWO * second_moment + (1.0 - BETA_TWO) * clipped * clipped
    fix_one = 1.0 - jnp.power(BETA_ONE, step)
    fix_two = 1.0 - jnp.power(BETA_TWO, step)
    motion = (
        new_first / fix_one / (jnp.sqrt(new_second / fix_two) + ADAM_EPS) + WEIGHT_DECAY * adapters
    )
    new_adapters = adapters - LEARN_RATE * motion
    return (loss, grad_norm, new_adapters, new_first, new_second, new_adapters.astype(jnp.bfloat16))


def solution(mesh):
    in_specs = (
        P(("vocab", "dp")),
        P(("vocab", "dp")),
        P(("vocab", "dp")),
        P(("vocab", "dp")),
        P("vocab", None),
        P(),
        P(),
        P(),
        P(),
        P(),
        P(),
        P(),
        P(),
        P(None, "vocab"),
        P(None, "vocab"),
        P(None, "vocab"),
        P(),
    )
    out_specs = (P(), P(), P(None, "vocab"), P(None, "vocab"), P(None, "vocab"), P(None, "vocab"))
    return jax.shard_map(local, mesh=mesh, in_specs=in_specs, out_specs=out_specs, check_vma=False)
```

profile of v0, /device:TPU:0, one launch (start us, length us, event | category | flops | bytes accessed | tf_op | source)
XLA Modules:
  0.0 552.6 jit_solution(14179724216567743253)
XLA Ops:
  7.2 10.7 %all-gather.1 = s32[8,1,256]{2,1,0:T(1,128)S(1)} all-gather(s32[1,1,256]{2,1,0:T(1,128)} %bitcast.172), channel_id=1, replica_groups=mesh['vocab'=8,'dp'=4] {'vocab'}, dimensions={0}, use_global_device_ids=true | all-gather | bytes 9216 | tf_op jit(solution)/shard_map/all_gather | solution.py:149
  18.0 17.3 %gather_fusion = bf16[2048,1024]{1,0:T(8,128)(2,1)} fusion(bf16[6288,1024]{1,0:T(8,128)(2,1)} %param.21, s32[2048]{0:T(1024)S(1)} %fusion.86), kind=kCustom, calls=%fused_computation | custom fusion | bytes 8396800 | tf_op jit(solution)/shard_map/jit(_take)/gather | solution.py:156
  35.3 4.1 select_convert_fusion
  39.5 0.6 copy-done.24
  40.3 0.3 reduce-window.9
  40.7 9.5 %all_gather.17 = bf16[1,24576]{1,0:T(2,128)(2,1)S(1)} all-gather(bf16[1,3072]{1,0:T(2,128)(2,1)S(1)} %convert_element_type.95), channel_id=1, replica_groups=mesh['vocab'=8,'dp'=4] {'vocab'}, dimensions={1}, use_global_device_ids=true | all-gather | bytes 55296 | tf_op jit(solution)/shard_map/all_gather | solution.py:163
  50.6 0.6 reshape.269
  51.1 0.6 reshape.264
  51.9 3.5 gather_fusion.1
  55.7 35.3 %reduce-scatter.6.cloned.1.call-done = bf16[256,1024]{1,0:T(8,128)(2,1)} async-done(((bf16[2048,1024]{1,0:T(8,128)(2,1)}), bf16[256,1024]{1,0:T(8,128)(2,1)}) %reduce-scatter.6.cloned.1.call-update) | async-done | bytes 524304 | tf_op jit(solution)/shard_map/reduce_scatter | solution.py:157
  90.9 1.3 fusion.77
  92.2 1.3 multiply_reduce_fusion.5
  93.6 1.3 add_convert_fusion.3
  95.1 4.6 fusion.27
  99.8 0.6 fusion.30
  100.4 1.2 fusion.107
  101.6 1.2 copy.47
  102.9 2.2 copy.46
  105.1 2.0 copy.45
  107.1 1.9 select_reduce_fusion.1
  109.1 0.9 fusion.33
  110.0 1.2 fusion.71
  111.6 0.7 fusion.54
  112.3 0.4 fusion.111
  112.8 0.2 multiply_reduce_fusion.4
  113.1 1.6 slice-done.5
  114.7 2.6 fusion.17
  117.4 2.8 fusion.112
  120.5 1.1 add_convert_fusion.1
  121.7 8.9 %all-gather = s32[8,1,256]{2,1,0:T(1,128)S(1)} all-gather(s32[1,1,256]{2,1,0:T(1,128)S(1)} %bitcast.173), channel_id=1, replica_groups=mesh['vocab'=8,'dp'=4] {'vocab'}, dimensions={0}, use_global_device_ids=true | all-gather | bytes 9216 | tf_op jit(solution)/shard_map/all_gather | solution.py:151
  130.6 8.1 %all-gather.2 = s32[8,1,256]{2,1,0:T(1,128)S(1)} all-gather(s32[1,1,256]{2,1,0:T(1,128)S(1)} %bitcast.174), channel_id=1, replica_groups=mesh['vocab'=8,'dp'=4] {'vocab'}, dimensions={0}, use_global_device_ids=true | all-gather | bytes 9216 | tf_op jit(solution)/shard_map/all_gather | solution.py:150
  138.7 19.6 %all-gather.5.cloned.1.call-done = bf16[2048,1024]{1,0:T(8,128)(2,1)} async-done(((bf16[256,1024]{1,0:T(8,128)(2,1)}), bf16[2048,1024]{1,0:T(8,128)(2,1)}) %all-gather.5.cloned.1.call-update) | async-done | bytes 4194320 | tf_op jit(solution)/shard_map/all_gather | solution.py:226
  158.3 35.7 %select_reduce_fusion = (f32[2048]{0:T(1024)S(1)}, f32[2048,6288]{0,1:T(8,128)}) fusion(pred[6288]{0:T(1024)(128)(4,1)S(1)} %broadcast_compare_fusion, bf16[2048,1024]{1,0:T(8,128)(2,1)} %all-gather.5.cloned.1.call-done, bf16[6288,1024]{1,0:T(8,128)(2,1)} %param.21), kind=kOutput, calls=%fused_computation.10 | convolution fusion | flops 26399537152 | bytes 68597904 | tf_op jit(solution)/shard_map/td,vd->tv/dot_general | solution.py:223
  194.1 13.3 %pmax.7 = f32[2048]{0:T(1024)S(1)} all-reduce(f32[2048]{0:T(1024)S(1)} %get-tuple-element.38), channel_id=1, replica_groups=mesh['vocab'=8,'dp'=4] {'vocab'}, use_global_device_ids=true, to_apply=%region_12.13 | all-reduce | flops 2048 | bytes 16384 | tf_op jit(solution)/shard_map/pmax | solution.py:233
  207.4 20.5 %fusion = (f32[2048]{0:T(1024)S(1)}, f32[2048]{0:T(1024)S(1)}) fusion(f32[2048,6288]{0,1:T(8,128)} %get-tuple-element.39, s32[2048]{0:T(1024)S(1)} %bitcast.159, s32[6288]{0:T(1024)S(1)} %iota_add_fusion, pred[6288]{0:T(1024)(128)(4,1)S(1)} %broadcast_compare_fusion, f32[2048]{0:T(1024)S(1)} %get-tuple-element.38), kind=kLoop, calls=%fused_computation.4 | loop fusion | flops 77262848 | bytes 51575504 | tf_op jit(solution)/shard_map/reduce_sum | solution.py:231
  227.9 12.3 %psum.35 = f32[2048]{0:T(1024)S(1)} all-reduce(f32[2048]{0:T(1024)S(1)} %exponential_multiply_fusion), channel_id=1, replica_groups=mesh['vocab'=8,'dp'=4] {'vocab'}, use_global_device_ids=true, to_apply=%region_14.15 | all-reduce | flops 2048 | bytes 16384 | tf_op jit(solution)/shard_map/psum | solution.py:235
  240.2 52.9 %fusion.5 = f32[2048,1024]{1,0:T(8,128)} fusion(bf16[6288,1024]{1,0:T(8,128)(2,1)} %param.21, f32[2048,6288]{0,1:T(8,128)} %get-tuple-element.39, f32[2048]{0:T(1024)S(1)} %log_add_fusion.1, f32[2048]{0:T(1024)S(1)} %bitcast.161, s32[2048]{0:T(1024)S(1)} %bitcast.160, s32[6288]{0:T(1024)S(1)} %iota_add_fusion, pred[6288]{0:T(1024)(128)(4,1)S(1)} %broadcast_compare_fusion), kind=kOutput, calls=%fused_computation.11 | convolution fusion | flops 26476806144 | bytes 72833744 | tf_op jit(solution)/shard_map/dot_general | solution.py:25
  293.2 71.7 %reduce-scatter.8.cloned.1.call-done = f32[256,1024]{1,0:T(8,128)} async-done(((f32[2048,1024]{1,0:T(8,128)}), f32[256,1024]{1,0:T(8,128)}) %reduce-scatter.8.cloned.1.call-update) | async-done | bytes 1048592 | tf_op jit(solution)/shard_map/reduce_scatter | solution.py:245
  364.9 1.5 multiply_reduce_fusion.6
  366.5 14.4 %fusion.104 = (f32[256]{0:T(256)S(1)}, f32[256]{0:T(256)S(1)}, f32[256,1024]{1,0:T(8,128)}) fusion(f32[256]{0:T(256)S(1)} %add_rsqrt_fusion.1, f32[256,1024]{1,0:T(8,128)} %copy-done.3, f32[256]{0:T(256)S(1)} %broadcast_multiply_fusion.5, f32[1024]{0:T(1024)S(1)} %bitcast.169, bf16[1,1024,4096]{2,1,0:T(8,128)(2,1)} %param.28, f32[256,4096]{1,0:T(8,128)} %copy-done.33, ...), kind=kOutput, calls=%fused_computation.162 | convolution fusion | flops 4323803136 | bytes 25182208 | tf_op jit(solution)/shard_map/tf,df->td/dot_general | solution.py:272
  380.9 2.5 add_convert_fusion
  383.8 0.7 fusion.37
  384.6 1.4 fusion.118
  386.0 1.5 fusion.68
  387.5 1.2 copy.49
  388.7 3.2 fusion.72
  392.2 1.4 multiply_reduce_fusion
  393.6 1.2 multiply_convert_fusion
  394.8 0.8 fusion.70
  395.5 0.5 fusion.69
  396.0 0.3 convolution_multiply_fusion.6
  396.4 0.5 fusion.75
  397.1 0.3 reshape.276
  397.4 0.7 fusion.117
  398.1 0.3 reshape.275
  398.4 6.8 %copy.61 = f32[1,24576]{0,1:T(8,128)} copy(f32[1,24576]{1,0:T(1,128)S(1)} %bitcast.147) | data formatting | bytes 196608
  405.9 91.7 %reduce-scatter.10.cloned.1.call-done = f32[3072,1]{1,0:T(8,128)} async-done(((f32[24576,1]{1,0:T(8,128)}), f32[3072,1]{1,0:T(8,128)}) %reduce-scatter.10.cloned.1.call-update) | async-done | bytes 12304
  497.6 1.9 copy.62
  499.5 18.7 %psum.38 = f32[1,3072]{1,0:T(1,128)S(1)} all-reduce(f32[1,3072]{1,0:T(1,128)S(1)} %copy.62), channel_id=1, replica_groups=mesh['vocab'=8,'dp'=4] {'dp'}, use_global_device_ids=true, to_apply=%region_26.27 | all-reduce | flops 3072 | bytes 24576 | tf_op jit(solution)/shard_map/psum | solution.py:315
  518.2 0.6 multiply_reduce_fusion.7
  518.8 13.0 %all-reduce = (f32[2048]{0:T(1024)S(1)}, f32[]{:T(128)}) all-reduce(f32[2048]{0:T(1024)S(1)} %get-tuple-element.6, f32[]{:T(128)} %multiply_reduce_fusion.7), channel_id=1, replica_groups=mesh['vocab'=8,'dp'=4] {'vocab'}, use_global_device_ids=true, to_apply=%region_16.17 | all-reduce | flops 2049 | bytes 16392 | tf_op jit(solution)/shard_map/psum | solution.py:235
  531.8 0.6 multiply_reduce_fusion.8
  533.1 9.0 %psum.37 = f32[]{:T(128)} all-reduce(f32[]{:T(128)} %multiply_reduce_fusion.8), channel_id=1, replica_groups=mesh['vocab'=8,'dp'=4] {'dp'}, use_global_device_ids=true, to_apply=%region_18.19 | all-reduce | flops 1 | bytes 8 | tf_op jit(solution)/shard_map/psum | solution.py:315
  542.8 0.7 fusion.105
  (133 shorter events, 3.1 us)
Async XLA Ops:
  7.2 104.3 %copy-start = (bf16[1,1024,1024]{2,1,0:T(8,128)(2,1)S(1)}, bf16[1,1024,1024]{2,1,0:T(8,128)(2,1)}, u32[]{:S(2)}) copy-start(bf16[1,1024,1024]{2,1,0:T(8,128)(2,1)} %param.27) | copy-start | bytes 6291460
  7.2 83.8 %reduce-scatter.6.cloned.1.call-start = ((), (), s32[]{:S(2)}) async-start(), calls=%async_computation.3 | async-start | bytes 4718592 | tf_op jit(solution)/shard_map/reduce_scatter | solution.py:157
  39.4 0.7 copy-start.24
  39.4 1.3 copy-start.21
  39.4 16.0 %copy-start.23 = (f32[1,9216]{1,0:T(1,128)S(1)}, f32[1,9216]{1,0:T(1,128)}, u32[]{:S(2)}) copy-start(f32[1,9216]{1,0:T(1,128)} %param.25) | copy-start | bytes 110596
  39.4 16.1 %copy-start.27 = (f32[3,1024]{1,0:T(4,128)S(1)}, f32[3,1024]{1,0:T(4,128)}, u32[]{:S(2)}) copy-start(f32[3,1024]{1,0:T(4,128)} %param.23) | copy-start | bytes 36868
  39.4 16.1 %copy-start.28 = (f32[3,1024]{1,0:T(4,128)S(1)}, f32[3,1024]{1,0:T(4,128)}, u32[]{:S(2)}) copy-start(f32[3,1024]{1,0:T(4,128)} %param.24) | copy-start | bytes 36868
  39.5 118.9 %all-gather.5.cloned.1.call-start = ((), (), s32[]{:S(2)}) async-start(), calls=%async_computation.4 | async-start | bytes 4718592 | tf_op jit(solution)/shard_map/all_gather | solution.py:226
  50.4 49.4 %copy-start.19 = (bf16[4,3072]{1,0:T(4,128)(2,1)}, bf16[4,3072]{1,0:T(4,128)(2,1)S(1)}, u32[]{:S(2)}) copy-start(bf16[4,3072]{1,0:T(4,128)(2,1)S(1)} %reshape.265) | copy-start | bytes 73732
  51.1 60.1 %copy-start.12 = (bf16[1024,4]{1,0:T(8,128)(2,1)}, bf16[1024,4]{1,0:T(8,128)(2,1)S(1)}, u32[]{:S(2)}) copy-start(bf16[1024,4]{1,0:T(8,128)(2,1)S(1)} %reshape.269) | copy-start | bytes 24580
  51.9 43.2 %slice-start = ((f32[1,9216]{1,0:T(1,128)}), f32[1,3072]{1,0:T(1,128)S(1)}, s32[]{:S(2)}) async-start(f32[1,9216]{1,0:T(1,128)} %param.25), calls=%async_computation.7 | async-start | bytes 24576 | tf_op jit(solution)/shard_map/slice | solution.py:179
  55.7 54.3 %copy-start.17 = (pred[256,256]{0,1:T(8,128)(4,1)}, pred[256,256]{0,1:T(8,128)(4,1)S(1)}, u32[]{:S(2)}) copy-start(pred[256,256]{0,1:T(8,128)(4,1)S(1)} %fusion.84) | copy-start | bytes 196612
  94.9 4.9 copy-start.7
  95.1 4.7 copy-start.29
  102.9 7.1 %copy-start.9 = (bf16[256,1024]{0,1:T(8,128)(2,1)}, bf16[256,1024]{0,1:T(8,128)(2,1)S(1)}, u32[]{:S(2)}) copy-start(bf16[256,1024]{0,1:T(8,128)(2,1)S(1)} %copy.47) | copy-start | bytes 1572868
  107.1 2.9 copy-start.14
  109.1 2.2 copy-start.1
  110.0 3.1 slice-start.4
  110.0 1.6 copy-start.4
  110.0 4.7 slice-start.5
  111.2 1.8 copy-start.5
  111.3 3.4 slice-start.1
  112.3 5.1 slice-start.2
  112.8 4.6 copy-start.3
  114.7 2.7 slice-start.3
  117.3 2.9 copy-start.33
  117.4 4.3 copy-start.31
  117.4 13.2 %copy-start.32 = (s32[256]{0:T(256)S(1)}, s32[256]{0:T(256)}, u32[]{:S(2)}) copy-start(s32[256]{0:T(256)} %param.18) | copy-start | bytes 3076
  121.6 243.3 %reduce-scatter.8.cloned.1.call-start = ((), (), s32[]{:S(2)}) async-start(), calls=%async_computation.5 | async-start | bytes 9437184 | tf_op jit(solution)/shard_map/reduce_scatter | solution.py:245
  293.1 204.5 %reduce-scatter.10.cloned.1.call-start = ((), (), s32[]{:S(2)}) async-start(), calls=%async_computation.6 | async-start | bytes 14155776
  380.9 3.7 copy-start.6
  380.9 5.1 copy-start.13
  383.6 5.1 copy-start.18
  386.0 6.0 %copy-start.15 = (bf16[256,1024]{0,1:T(8,128)(2,1)S(1)}, bf16[256,1024]{0,1:T(8,128)(2,1)}, u32[]{:S(2)}) copy-start(bf16[256,1024]{0,1:T(8,128)(2,1)} %copy.45) | copy-start | bytes 1572868
  388.7 3.5 copy-start.2
  393.5 1.2 copy-start.11
  393.5 2.0 copy-start.10
  394.8 1.3 copy-start.20
  395.5 0.8 copy-start.30
  396.0 1.0 copy-start.16
  396.0 1.3 copy-start.8
  405.1 137.7 %copy-start.22 = (f32[1,3072]{1,0:T(1,128)S(1)}, f32[1,3072]{1,0:T(1,128)}, u32[]{:S(2)}) copy-start(f32[1,3072]{1,0:T(1,128)} %param.30) | copy-start | bytes 36868
  405.1 137.7 %copy-start.25 = (f32[1,3072]{1,0:T(1,128)S(1)}, f32[1,3072]{1,0:T(1,128)}, u32[]{:S(2)}) copy-start(f32[1,3072]{1,0:T(1,128)} %param.32) | copy-start | bytes 36868
  405.1 137.7 %copy-start.26 = (f32[1,3072]{1,0:T(1,128)S(1)}, f32[1,3072]{1,0:T(1,128)}, u32[]{:S(2)}) copy-start(f32[1,3072]{1,0:T(1,128)} %param.31) | copy-start | bytes 36868
Sparse Core Ops, SparseCore 0:
  39.6 51.2 reduce-scatter.5
  121.7 36.5 all-gather.4
  293.3 71.5 reduce-scatter.7
  405.3 92.2 reduce-scatter.9
where the time goes:
time: 557 us; the launch traced here: 553 us
  waiting for transfers between devices  218 us (39%)
  matrix products  130 us (23%)
  blocking collectives  104 us (19%)
  local copies, waits for them, and re-layouts  42.4 us (8%)
  other arithmetic  39 us (7%)
  between operations  19.2 us (3%)
    unnamed x5, waiting for transfers between devices  91.8 us
    reduce_scatter x1, waiting for transfers between devices, local(): lax.psum_scatter(mixed_product(grad_logits, embed_table), 'vocab', scatte...  71.7 us
    dot_general x9, matrix products, mixed_product(): return jnp.dot(left, right, preferred_element_type=jnp.float32)  65.3 us
    dot_general x1, matrix products, head_logits(): jnp.einsum('td,vd->tv', row_block, embed_table, preferred_element_type=jn...  35.7 us
    reduce_scatter x1, waiting for transfers between devices, local(): lax.psum_scatter(jnp.where(inside[:, None], picked_rows.astype(jnp.float3...  35.3 us
    psum x2, blocking collectives, local(): grad_shard, loss_sum = lax.psum((grad_shard, loss_part), 'dp')  27.7 us
    psum x2, blocking collectives, local(): row_total, picked = lax.psum((row_total, picked), 'vocab')  25.3 us
    reduce_sum x1, other arithmetic, local(): jnp.sum(jnp.where(columns[None, :] == wanted[:, None], logits, 0.0), -1)  20.5 us
  transfers between devices with their start and end apart: 4, of which 4 were waited for; matrix products, arithmetic and copies ran while one was open for 1% of the time, Pallas kernels for 0%

commit v1 on v0

--- a/solution.py
+++ b/solution.py
@@ -19,6 +19,24 @@
 ADAM_EPS = 1e-08
 WEIGHT_DECAY = 0.01
 LEARN_RATE = 0.02
+
+
+def gather_around(value, axis, dim):
+    ways, here, lap = (lax.axis_size(axis), lax.axis_index(axis), value.shape[dim])
+    dims = [n * ways if d == dim else n for d, n in enumerate(value.shape)]
+    full = lax.dynamic_update_slice_in_dim(
+        jnp.zeros(dims, value.dtype), value, here * lap, axis=dim
+    )
+    going_up = going_down = value
+    for far in range(1, ways // 2 + 1):
+        going_up = lax.ppermute(going_up, axis, [(d, (d + 1) % ways) for d in range(ways)])
+        full = lax.dynamic_update_slice_in_dim(full, going_up, (here - far) % ways * lap, axis=dim)
+        if 2 * far < ways:
+            going_down = lax.ppermute(going_down, axis, [(d, (d - 1) % ways) for d in range(ways)])
+            full = lax.dynamic_update_slice_in_dim(
+                full, going_down, (here + far) % ways * lap, axis=dim
+            )
+    return full
 
 
 def mixed_product(left, right):
@@ -223,7 +241,7 @@
         logits = jnp.einsum("td,vd->tv", row_block, embed_table, preferred_element_type=jnp.float32)
         return jnp.where(live[None], logits, -1e30)
 
-    piece = lax.all_gather(hidden, "vocab", axis=0, tiled=True)
+    piece = gather_around(hidden, "vocab", 0)
     logits = head_logits(piece)
     row_top = jnp.max(logits, -1)
     row_total = jnp.sum(jnp.exp(logits - row_top[:, None]), -1)

time: 557 us -> 587 us (1.054)
  local copies, waits for them, and re-layouts: 42.4 us -> 56.9 us
  waiting for transfers between devices: 218 us -> 225 us
  starting transfers between devices: 0.16 us -> 6.89 us
    ppermute x0 -> x7, waiting for transfers between devices: none -> 27.3 us  [the longest x4 26 us: gather_around(): lax.ppermute(going_up, axis, [(d, (d + 1) % ways) for d in range(ways)])]
    all_gather x1 -> x0, waiting for transfers between devices: 19.6 us -> none  [local(): piece = lax.all_gather(hidden, 'vocab', axis=0, tiled=True)]
    dynamic_update_slice x0 -> x7, local copies, waits for them, and re-layouts: none -> 11.1 us  [the longest x4 6.51 us: gather_around(): lax.dynamic_update_slice_in_dim(full, going_up, (here - far) % ways * lap...]
    ppermute x0 -> x7, starting transfers between devices: none -> 6.76 us  [the longest x3 6.75 us: gather_around(): lax.ppermute(going_down, axis, [(d, (d - 1) % ways) for d in range(ways)])]
    unnamed x80 -> x86, local copies, waits for them, and re-layouts: 11.5 us -> 12.3 us
    unnamed x5 -> x4, waiting for transfers between devices: 91.8 us -> 91.7 us
  transfers between devices with their start and end apart: 4 -> 10, of which waited for: 4 -> 7; matrix products, arithmetic and copies ran while one was open for 1% -> 3% of each run, Pallas kernels for 0% -> 0%
where the time goes in v1:
time: 587 us; the launch traced here: 583 us
  waiting for transfers between devices  225 us (38%)
  matrix products  130 us (22%)
  blocking collectives  106 us (18%)
  local copies, waits for them, and re-layouts  56.9 us (10%)
  other arithmetic  39 us (7%)
  between operations  19.3 us (3%)
  starting transfers between devices  6.89 us (1%)
    unnamed x4, waiting for transfers between devices  91.7 us
    reduce_scatter x1, waiting for transfers between devices, local(): lax.psum_scatter(mixed_product(grad_logits, embed_table), 'vocab', scatte...  70.9 us
    dot_general x9, matrix products, mixed_product(): return jnp.dot(left, right, preferred_element_type=jnp.float32)  65.3 us
    dot_general x1, matrix products, head_logits(): jnp.einsum('td,vd->tv', row_block, embed_table, preferred_element_type=jn...  35.7 us
    reduce_scatter x1, waiting for transfers between devices, local(): lax.psum_scatter(jnp.where(inside[:, None], picked_rows.astype(jnp.float3...  35.3 us
    psum x2, blocking collectives, local(): grad_shard, loss_sum = lax.psum((grad_shard, loss_part), 'dp')  27.7 us
    ppermute x4, waiting for transfers between devices, gather_around(): lax.ppermute(going_up, axis, [(d, (d + 1) % ways) for d in range(ways)])  26 us
    psum x2, blocking collectives, local(): row_total, picked = lax.psum((row_total, picked), 'vocab')  25.3 us
  transfers between devices with their start and end apart: 10, of which 7 were waited for; matrix products, arithmetic and copies ran while one was open for 3% of the time, Pallas kernels for 0%

profile of v1, /device:TPU:0, one launch (start us, length us, event | category | flops | bytes accessed | tf_op | source)
XLA Modules:
  0.0 582.7 jit_solution(2534361294629523034)
XLA Ops:
  7.2 10.7 %all-gather.1 = s32[8,1,256]{2,1,0:T(1,128)S(1)} all-gather(s32[1,1,256]{2,1,0:T(1,128)} %bitcast.172), channel_id=1, replica_groups=mesh['vocab'=8,'dp'=4] {'vocab'}, dimensions={0}, use_global_device_ids=true | all-gather | bytes 9216 | tf_op jit(solution)/shard_map/all_gather | solution.py:167
  18.0 17.3 %gather_fusion = bf16[2048,1024]{1,0:T(8,128)(2,1)} fusion(bf16[6288,1024]{1,0:T(8,128)(2,1)} %param.21, s32[2048]{0:T(1024)S(1)} %fusion.86), kind=kCustom, calls=%fused_computation | custom fusion | bytes 8396800 | tf_op jit(solution)/shard_map/jit(_take)/gather | solution.py:174
  35.3 4.1 select_convert_fusion
  40.7 9.5 %all_gather.14 = bf16[1,24576]{1,0:T(2,128)(2,1)S(1)} all-gather(bf16[1,3072]{1,0:T(2,128)(2,1)S(1)} %convert_element_type.95), channel_id=1, replica_groups=mesh['vocab'=8,'dp'=4] {'vocab'}, dimensions={1}, use_global_device_ids=true | all-gather | bytes 55296 | tf_op jit(solution)/shard_map/all_gather | solution.py:181
  51.9 3.5 gather_fusion.1
  55.7 35.3 %reduce-scatter.6.cloned.1.call-done = bf16[256,1024]{1,0:T(8,128)(2,1)} async-done(((bf16[2048,1024]{1,0:T(8,128)(2,1)}), bf16[256,1024]{1,0:T(8,128)(2,1)}) %reduce-scatter.6.cloned.1.call-update) | async-done | bytes 524304 | tf_op jit(solution)/shard_map/reduce_scatter | solution.py:175
  90.9 1.3 fusion.77
  92.2 1.3 multiply_reduce_fusion.5
  93.6 1.3 add_convert_fusion.3
  95.1 4.6 fusion.27
  100.4 1.2 fusion.107
  101.6 1.2 copy.47
  102.9 2.2 copy.46
  105.1 2.0 copy.45
  107.1 1.9 select_reduce_fusion.1
  109.1 0.9 fusion.33
  110.0 1.2 fusion.71
  111.6 0.7 fusion.54
  113.1 1.6 slice-done.5
  114.7 2.6 fusion.17
  117.4 2.8 fusion.112
  120.5 2.6 broadcast_in_dim.106
  123.1 1.1 constant_dynamic-update-slice_fusion.7
  124.2 2.6 collective-permute-start.1
  126.8 11.6 %collective-permute-done = bf16[256,1024]{1,0:T(8,128)(2,1)S(1)} collective-permute-done((bf16[256,1024]{1,0:T(8,128)(2,1)S(1)}, bf16[256,1024]{1,0:T(8,128)(2,1)S(1)}, u32[]{:S(2)}, u32[]{:S(2)}) %collective-permute-start) | collective-permute-done | bytes 524320 | tf_op jit(solution)/shard_map/ppermute | solution.py:32
  138.4 0.8 copy-done.19
  139.2 2.6 collective-permute-start.3
  141.9 12.3 %collective-permute-done.2 = bf16[256,1024]{1,0:T(8,128)(2,1)} collective-permute-done((bf16[256,1024]{1,0:T(8,128)(2,1)S(1)}, bf16[256,1024]{1,0:T(8,128)(2,1)}, u32[]{:S(2)}, u32[]{:S(2)}) %collective-permute-start.2) | collective-permute-done | bytes 524320 | tf_op jit(solution)/shard_map/ppermute | solution.py:32
  154.1 10.5 %all-gather = s32[8,1,256]{2,1,0:T(1,128)S(1)} all-gather(s32[1,1,256]{2,1,0:T(1,128)S(1)} %bitcast.173), channel_id=1, replica_groups=mesh['vocab'=8,'dp'=4] {'vocab'}, dimensions={0}, use_global_device_ids=true | all-gather | bytes 9216 | tf_op jit(solution)/shard_map/all_gather | solution.py:169
  164.7 9.2 %all-gather.2 = s32[8,1,256]{2,1,0:T(1,128)S(1)} all-gather(s32[1,1,256]{2,1,0:T(1,128)S(1)} %bitcast.174), channel_id=1, replica_groups=mesh['vocab'=8,'dp'=4] {'vocab'}, dimensions={0}, use_global_device_ids=true | all-gather | bytes 9216 | tf_op jit(solution)/shard_map/all_gather | solution.py:168
  174.0 1.5 collective-permute-start.5
  175.4 1.9 constant_dynamic-update-slice_fusion.6
  177.3 1.9 constant_dynamic-update-slice_fusion.5
  179.2 1.9 constant_dynamic-update-slice_fusion.4
  181.1 1.9 constant_dynamic-update-slice_fusion.3
  183.0 1.9 constant_dynamic-update-slice_fusion.2
  184.9 1.3 collective-permute-done.5
  186.2 0.8 constant_dynamic-update-slice_fusion.1
  187.0 2.2 collective-permute-done.6
  189.2 0.8 constant_dynamic-update-slice_fusion
  190.0 35.7 %select_reduce_fusion = (f32[2048]{0:T(1024)S(1)}, f32[2048,6288]{0,1:T(8,128)}) fusion(pred[6288]{0:T(1024)(128)(4,1)S(1)} %broadcast_compare_fusion, bf16[2048,1024]{1,0:T(8,128)(2,1)} %constant_dynamic-update-slice_fusion, bf16[6288,1024]{1,0:T(8,128)(2,1)} %param.21), kind=kOutput, calls=%fused_computation.10 | convolution fusion | flops 26399537152 | bytes 68597904 | tf_op jit(solution)/shard_map/td,vd->tv/dot_general | solution.py:241
  225.7 12.6 %pmax.7 = f32[2048]{0:T(1024)S(1)} all-reduce(f32[2048]{0:T(1024)S(1)} %get-tuple-element.40), channel_id=1, replica_groups=mesh['vocab'=8,'dp'=4] {'vocab'}, use_global_device_ids=true, to_apply=%region_12.13 | all-reduce | flops 2048 | bytes 16384 | tf_op jit(solution)/shard_map/pmax | solution.py:251
  238.3 20.5 %fusion = (f32[2048]{0:T(1024)S(1)}, f32[2048]{0:T(1024)S(1)}) fusion(f32[2048,6288]{0,1:T(8,128)} %get-tuple-element.41, s32[2048]{0:T(1024)S(1)} %bitcast.159, s32[6288]{0:T(1024)S(1)} %iota_add_fusion, pred[6288]{0:T(1024)(128)(4,1)S(1)} %broadcast_compare_fusion, f32[2048]{0:T(1024)S(1)} %get-tuple-element.40), kind=kLoop, calls=%fused_computation.4 | loop fusion | flops 77262848 | bytes 51575504 | tf_op jit(solution)/shard_map/reduce_sum | solution.py:249
  258.8 12.3 %psum.35 = f32[2048]{0:T(1024)S(1)} all-reduce(f32[2048]{0:T(1024)S(1)} %exponential_multiply_fusion), channel_id=1, replica_groups=mesh['vocab'=8,'dp'=4] {'vocab'}, use_global_device_ids=true, to_apply=%region_14.15 | all-reduce | flops 2048 | bytes 16384 | tf_op jit(solution)/shard_map/psum | solution.py:253
  271.1 53.0 %fusion.5 = f32[2048,1024]{1,0:T(8,128)} fusion(bf16[6288,1024]{1,0:T(8,128)(2,1)} %param.21, f32[2048,6288]{0,1:T(8,128)} %get-tuple-element.41, f32[2048]{0:T(1024)S(1)} %log_add_fusion.1, f32[2048]{0:T(1024)S(1)} %bitcast.161, s32[2048]{0:T(1024)S(1)} %bitcast.160, s32[6288]{0:T(1024)S(1)} %iota_add_fusion, pred[6288]{0:T(1024)(128)(4,1)S(1)} %broadcast_compare_fusion), kind=kOutput, calls=%fused_computation.11 | convolution fusion | flops 26476806144 | bytes 72833744 | tf_op jit(solution)/shard_map/dot_general | solution.py:43
  324.2 70.9 %reduce-scatter.8.cloned.1.call-done = f32[256,1024]{1,0:T(8,128)} async-done(((f32[2048,1024]{1,0:T(8,128)}), f32[256,1024]{1,0:T(8,128)}) %reduce-scatter.8.cloned.1.call-update) | async-done | bytes 1048592 | tf_op jit(solution)/shard_map/reduce_scatter | solution.py:263
  395.0 1.5 multiply_reduce_fusion.6
  396.6 14.4 %fusion.104 = (f32[256]{0:T(256)S(1)}, f32[256]{0:T(256)S(1)}, f32[256,1024]{1,0:T(8,128)}) fusion(f32[256]{0:T(256)S(1)} %add_rsqrt_fusion.1, f32[256,1024]{1,0:T(8,128)} %copy-done.3, f32[256]{0:T(256)S(1)} %broadcast_multiply_fusion.5, f32[1024]{0:T(1024)S(1)} %bitcast.169, bf16[1,1024,4096]{2,1,0:T(8,128)(2,1)} %param.28, f32[256,4096]{1,0:T(8,128)} %copy-done.36, ...), kind=kOutput, calls=%fused_computation.170 | convolution fusion | flops 4323803136 | bytes 25182208 | tf_op jit(solution)/shard_map/tf,df->td/dot_general | solution.py:290
  411.0 2.5 add_convert_fusion
  414.0 0.7 fusion.37
  414.7 1.4 fusion.118
  416.1 1.5 fusion.68
  417.6 1.2 copy.49
  418.9 3.2 fusion.72
  422.3 1.4 multiply_reduce_fusion
  423.7 1.2 multiply_convert_fusion
  424.9 0.8 fusion.70
  428.5 6.8 %copy.61 = f32[1,24576]{0,1:T(8,128)} copy(f32[1,24576]{1,0:T(1,128)S(1)} %bitcast.147) | data formatting | bytes 196608
  436.0 91.7 %reduce-scatter.10.cloned.1.call-done = f32[3072,1]{1,0:T(8,128)} async-done(((f32[24576,1]{1,0:T(8,128)}), f32[3072,1]{1,0:T(8,128)}) %reduce-scatter.10.cloned.1.call-update) | async-done | bytes 12304
  527.7 1.9 copy.62
  529.6 18.7 %psum.38 = f32[1,3072]{1,0:T(1,128)S(1)} all-reduce(f32[1,3072]{1,0:T(1,128)S(1)} %copy.62), channel_id=1, replica_groups=mesh['vocab'=8,'dp'=4] {'dp'}, use_global_device_ids=true, to_apply=%region_26.27 | all-reduce | flops 3072 | bytes 24576 | tf_op jit(solution)/shard_map/psum | solution.py:333
  548.9 13.0 %all-reduce = (f32[2048]{0:T(1024)S(1)}, f32[]{:T(128)}) all-reduce(f32[2048]{0:T(1024)S(1)} %get-tuple-element.6, f32[]{:T(128)} %multiply_reduce_fusion.7), channel_id=1, replica_groups=mesh['vocab'=8,'dp'=4] {'vocab'}, use_global_device_ids=true, to_apply=%region_16.17 | all-reduce | flops 2049 | bytes 16392 | tf_op jit(solution)/shard_map/psum | solution.py:253
  563.2 9.0 %psum.37 = f32[]{:T(128)} all-reduce(f32[]{:T(128)} %multiply_reduce_fusion.8), channel_id=1, replica_groups=mesh['vocab'=8,'dp'=4] {'dp'}, use_global_device_ids=true, to_apply=%region_18.19 | all-reduce | flops 1 | bytes 8 | tf_op jit(solution)/shard_map/psum | solution.py:333
  573.0 0.7 fusion.105
  (158 shorter events, 10.2 us)
Async XLA Ops:
  7.2 104.3 %copy-start = (bf16[1,1024,1024]{2,1,0:T(8,128)(2,1)S(1)}, bf16[1,1024,1024]{2,1,0:T(8,128)(2,1)}, u32[]{:S(2)}) copy-start(bf16[1,1024,1024]{2,1,0:T(8,128)(2,1)} %param.27) | copy-start | bytes 6291460
  7.2 83.8 %reduce-scatter.6.cloned.1.call-start = ((), (), s32[]{:S(2)}) async-start(), calls=%async_computation.3 | async-start | bytes 4718592 | tf_op jit(solution)/shard_map/reduce_scatter | solution.py:175
  39.4 0.7 copy-start.27
  39.4 1.3 copy-start.22
  39.4 16.0 %copy-start.24 = (f32[1,9216]{1,0:T(1,128)S(1)}, f32[1,9216]{1,0:T(1,128)}, u32[]{:S(2)}) copy-start(f32[1,9216]{1,0:T(1,128)} %param.25) | copy-start | bytes 110596
  39.4 16.1 %copy-start.30 = (f32[3,1024]{1,0:T(4,128)S(1)}, f32[3,1024]{1,0:T(4,128)}, u32[]{:S(2)}) copy-start(f32[3,1024]{1,0:T(4,128)} %param.23) | copy-start | bytes 36868
  39.4 16.1 %copy-start.31 = (f32[3,1024]{1,0:T(4,128)S(1)}, f32[3,1024]{1,0:T(4,128)}, u32[]{:S(2)}) copy-start(f32[3,1024]{1,0:T(4,128)} %param.24) | copy-start | bytes 36868
  39.5 355.6 %reduce-scatter.8.cloned.1.call-start = ((), (), s32[]{:S(2)}) async-start(), calls=%async_computation.4 | async-start | bytes 9437184 | tf_op jit(solution)/shard_map/reduce_scatter | solution.py:263
  50.4 49.4 %copy-start.20 = (bf16[4,3072]{1,0:T(4,128)(2,1)}, bf16[4,3072]{1,0:T(4,128)(2,1)S(1)}, u32[]{:S(2)}) copy-start(bf16[4,3072]{1,0:T(4,128)(2,1)S(1)} %reshape.265) | copy-start | bytes 73732
  51.1 60.1 %copy-start.12 = (bf16[1024,4]{1,0:T(8,128)(2,1)}, bf16[1024,4]{1,0:T(8,128)(2,1)S(1)}, u32[]{:S(2)}) copy-start(bf16[1024,4]{1,0:T(8,128)(2,1)S(1)} %reshape.269) | copy-start | bytes 24580
  51.9 43.2 %slice-start = ((f32[1,9216]{1,0:T(1,128)}), f32[1,3072]{1,0:T(1,128)S(1)}, s32[]{:S(2)}) async-start(f32[1,9216]{1,0:T(1,128)} %param.25), calls=%async_computation.6 | async-start | bytes 24576 | tf_op jit(solution)/shard_map/slice | solution.py:197
  55.7 54.3 %copy-start.17 = (pred[256,256]{0,1:T(8,128)(4,1)}, pred[256,256]{0,1:T(8,128)(4,1)S(1)}, u32[]{:S(2)}) copy-start(pred[256,256]{0,1:T(8,128)(4,1)S(1)} %fusion.84) | copy-start | bytes 196612
  94.9 4.9 copy-start.7
  95.1 4.7 copy-start.32
  102.9 7.1 %copy-start.9 = (bf16[256,1024]{0,1:T(8,128)(2,1)}, bf16[256,1024]{0,1:T(8,128)(2,1)S(1)}, u32[]{:S(2)}) copy-start(bf16[256,1024]{0,1:T(8,128)(2,1)S(1)} %copy.47) | copy-start | bytes 1572868
  107.1 2.9 copy-start.14
  109.1 2.2 copy-start.1
  110.0 3.1 slice-start.4
  110.0 1.6 copy-start.4
  110.0 4.7 slice-start.5
  111.2 1.8 copy-start.5
  111.3 3.4 slice-start.1
  111.5 5.8 %copy-start.25 = (bf16[256,4]{0,1:T(4,128)(2,1)}, bf16[256,4]{0,1:T(4,128)(2,1)S(1)}, u32[]{:S(2)}) copy-start(bf16[256,4]{0,1:T(4,128)(2,1)S(1)} %convolution_convert_fusion) | copy-start | bytes 6148
  112.3 5.1 slice-start.2
  112.8 4.6 copy-start.3
  114.7 2.7 slice-start.3
  117.3 2.9 copy-start.36
  120.2 33.9 %copy-start.34 = (s32[256]{0:T(256)S(1)}, s32[256]{0:T(256)}, u32[]{:S(2)}) copy-start(s32[256]{0:T(256)} %param.19) | copy-start | bytes 3076
  120.2 44.4 %copy-start.35 = (s32[256]{0:T(256)S(1)}, s32[256]{0:T(256)}, u32[]{:S(2)}) copy-start(s32[256]{0:T(256)} %param.18) | copy-start | bytes 3076
  124.2 14.2 %collective-permute-start = (bf16[256,1024]{1,0:T(8,128)(2,1)S(1)}, bf16[256,1024]{1,0:T(8,128)(2,1)S(1)}, u32[]{:S(2)}, u32[]{:S(2)}) collective-permute-start(bf16[256,1024]{1,0:T(8,128)(2,1)S(1)} %get-tuple-element.22), channel_id=1, source_target_pairs={{0,4},{4,8},{8,12},{12,16},{16,20},{20,24},{24,28},{28,0},{1,5},{5... | collective-permute-start | bytes 1572872 | tf_op jit(solution)/shard_map/ppermute | solution.py:32
  124.2 15.1 %collective-permute-start.1 = (bf16[256,1024]{1,0:T(8,128)(2,1)S(1)}, bf16[256,1024]{1,0:T(8,128)(2,1)}, u32[]{:S(2)}, u32[]{:S(2)}) collective-permute-start(bf16[256,1024]{1,0:T(8,128)(2,1)S(1)} %get-tuple-element.22), channel_id=1, source_target_pairs={{0,28},{4,0},{8,4},{12,8},{16,12},{20,16},{24,20},{28,24},{1,29},{... | collective-permute-start | bytes 1572872 | tf_op jit(solution)/shard_map/ppermute | solution.py:35
  138.4 0.8 copy-start.19
  139.2 14.9 %collective-permute-start.2 = (bf16[256,1024]{1,0:T(8,128)(2,1)S(1)}, bf16[256,1024]{1,0:T(8,128)(2,1)}, u32[]{:S(2)}, u32[]{:S(2)}) collective-permute-start(bf16[256,1024]{1,0:T(8,128)(2,1)S(1)} %collective-permute-done), channel_id=1, source_target_pairs={{0,4},{4,8},{8,12},{12,16},{16,20},{20,24},{24,28},{28,0},{1,5},{5... | collective-permute-start | bytes 1572872 | tf_op jit(solution)/shard_map/ppermute | solution.py:32
  139.2 34.7 %collective-permute-start.3 = (bf16[256,1024]{1,0:T(8,128)(2,1)}, bf16[256,1024]{1,0:T(8,128)(2,1)}, u32[]{:S(2)}, u32[]{:S(2)}) collective-permute-start(bf16[256,1024]{1,0:T(8,128)(2,1)} %collective-permute-done.1), channel_id=1, source_target_pairs={{0,28},{4,0},{8,4},{12,8},{16,12},{20,16},{24,20},{28,24},{1,29},{... | collective-permute-start | bytes 1572872 | tf_op jit(solution)/shard_map/ppermute | solution.py:35
  154.1 23.2 %collective-permute-start.4 = (bf16[256,1024]{1,0:T(8,128)(2,1)}, bf16[256,1024]{1,0:T(8,128)(2,1)}, u32[]{:S(2)}, u32[]{:S(2)}) collective-permute-start(bf16[256,1024]{1,0:T(8,128)(2,1)} %collective-permute-done.2), channel_id=1, source_target_pairs={{0,4},{4,8},{8,12},{12,16},{16,20},{20,24},{24,28},{28,0},{1,5},{5... | collective-permute-start | bytes 1572872 | tf_op jit(solution)/shard_map/ppermute | solution.py:32
  174.0 12.2 %collective-permute-start.5 = (bf16[256,1024]{1,0:T(8,128)(2,1)}, bf16[256,1024]{1,0:T(8,128)(2,1)S(1)}, u32[]{:S(2)}, u32[]{:S(2)}) collective-permute-start(bf16[256,1024]{1,0:T(8,128)(2,1)} %collective-permute-done.3), channel_id=1, source_target_pairs={{0,28},{4,0},{8,4},{12,8},{16,12},{20,16},{24,20},{28,24},{1,29},{... | collective-permute-start | bytes 1572872 | tf_op jit(solution)/shard_map/ppermute | solution.py:35
  177.3 11.8 %collective-permute-start.6 = (bf16[256,1024]{1,0:T(8,128)(2,1)}, bf16[256,1024]{1,0:T(8,128)(2,1)S(1)}, u32[]{:S(2)}, u32[]{:S(2)}) collective-permute-start(bf16[256,1024]{1,0:T(8,128)(2,1)} %collective-permute-done.4), channel_id=1, source_target_pairs={{0,4},{4,8},{8,12},{12,16},{16,20},{20,24},{24,28},{28,0},{1,5},{5... | collective-permute-start | bytes 1572872 | tf_op jit(solution)/shard_map/ppermute | solution.py:32
  324.1 203.6 %reduce-scatter.10.cloned.1.call-start = ((), (), s32[]{:S(2)}) async-start(), calls=%async_computation.5 | async-start | bytes 14155776
  411.0 2.8 copy-start.26
  411.0 3.7 copy-start.6
  411.0 5.1 copy-start.13
  413.8 5.1 copy-start.18
  416.1 6.0 %copy-start.15 = (bf16[256,1024]{0,1:T(8,128)(2,1)S(1)}, bf16[256,1024]{0,1:T(8,128)(2,1)}, u32[]{:S(2)}) copy-start(bf16[256,1024]{0,1:T(8,128)(2,1)} %copy.45) | copy-start | bytes 1572868
  418.8 3.5 copy-start.2
  423.7 1.2 copy-start.11
  423.7 2.0 copy-start.10
  424.9 1.3 copy-start.21
  425.7 0.8 copy-start.33
  426.2 1.0 copy-start.16
  426.2 1.3 copy-start.8
  435.3 137.7 %copy-start.23 = (f32[1,3072]{1,0:T(1,128)S(1)}, f32[1,3072]{1,0:T(1,128)}, u32[]{:S(2)}) copy-start(f32[1,3072]{1,0:T(1,128)} %param.30) | copy-start | bytes 36868
  435.3 137.7 %copy-start.28 = (f32[1,3072]{1,0:T(1,128)S(1)}, f32[1,3072]{1,0:T(1,128)}, u32[]{:S(2)}) copy-start(f32[1,3072]{1,0:T(1,128)} %param.32) | copy-start | bytes 36868
  435.3 137.7 %copy-start.29 = (f32[1,3072]{1,0:T(1,128)S(1)}, f32[1,3072]{1,0:T(1,128)}, u32[]{:S(2)}) copy-start(f32[1,3072]{1,0:T(1,128)} %param.31) | copy-start | bytes 36868
Sparse Core Ops, SparseCore 0:
  39.6 51.2 reduce-scatter.5
  324.2 70.7 reduce-scatter.7
  435.4 92.2 reduce-scatter.9
